TPU v7x, 32 devices: a whole 2x2x4 slice. The times are simulated.
32 devices in a mesh: rows: 4 (over y, x), wide: 8 (over z, core).
Axes of the slice: x: 2, y: 2, z: 4, core: 2. Of those that a mesh axis runs over, the one named last changes fastest.
Arguments:
- tokens: bfloat16 [16, 1024, 1024], P('rows', 'wide'), may hold values from -6 to 6
- segments: int32 [16, 1024], P('rows'), may hold values from 0 to 15, never falling along the last dimension, each value on 1 to 128 neighbouring positions
- w_qkv: bfloat16 [2, 1024, 3072], replicated, may hold values from -0.1875 to 0.1875
- b_qkv: float32 [2, 3072], replicated, may hold values from -3 to 3
- w_out: bfloat16 [2, 1024, 1024], replicated, may hold values from -1 to 1
- b_out: float32 [2, 1024], replicated, may hold values from -3 to 3
- norm_gain: float32 [2, 2, 1024], replicated, may hold values from 0.5 to 1.5
- norm_bias: float32 [2, 2, 1024], replicated, may hold values from -2 to 2
- w_up: bfloat16 [2, 4096, 1024], P(None, 'wide'), may hold values from -0.1875 to 0.1875
- b_up: bfloat16 [2, 4096], P(None, 'wide'), may hold values from -3 to 3
- w_down: bfloat16 [2, 4096, 1024], P(None, 'wide'), may hold values from -0.09375 to 0.09375
- b_down: float32 [2, 1024], replicated, may hold values from -2 to 2
- prefix: bfloat16 [2, 2, 64, 1024], replicated, may hold values from -6 to 6
- cotangent: bfloat16 [16, 1024, 1024], P('rows', 'wide'), may hold values from -6 to 6
Outputs:
- output: bfloat16 [16, 1024, 1024], P('rows', 'wide')
- grad_tokens: float32 [16, 1024, 1024], P('rows', 'wide')
- grad_prefix: float32 [2, 2, 64, 1024], replicated
Inputs may be any that keep to these rules, and one draw needn't show every extreme that they name: `segments`: along each row the pair ids never fall, each pair covers 1 to 128 consecutive positions, and some pair covers exactly 128.
All inputs are finite; a program needn't handle non-finite values.
Results may differ from a plain program's by a relative error of at most 0.02.
Values may be sent and summed in bfloat16 or wider, within the bound.
A program may use at most 320 MiB of HBM per device.

v0:
```python
import math
import jax
import jax.numpy as jnp
from jax import lax
from jax.sharding import PartitionSpec as P

HEADS = 16
PAIR_MAX = 128
LAYERS = 2


def extended(block, sides, width):
    for axis, dim in sides:
        count = lax.axis_size(axis)
        forward = [(i, i + 1) for i in range(count - 1)]
        backward = [(target, source) for source, target in forward]
        low = lax.ppermute(
            lax.slice_in_dim(block, block.shape[dim] - width, None, axis=dim), axis, forward
        )
        high = lax.ppermute(lax.slice_in_dim(block, 0, width, axis=dim), axis, backward)
        block = jnp.concatenate([low, block, high], axis=dim)
    return block


def normalize(values, gain, shift):
    center = values - jnp.mean(values, axis=-1, keepdims=True)
    spread = jnp.mean(center * center, axis=-1, keepdims=True)
    return center * lax.rsqrt(spread + 1e-05) * gain + shift


def gelu_exact(values):
    return jax.nn.gelu(values, approximate=False)


def gelu_back(pre_values, grad_values):
    return jax.vjp(gelu_exact, pre_values)[1](grad_values)[0]


def norm_grad(values, gain, shift, grad_values):
    return jax.vjp(lambda inner: normalize(inner, gain, shift), values)[1](grad_values)[0]


def multiply(left, right):
    return jnp.dot(left, right, preferred_element_type=jnp.float32)


def multiply_back(left, right):
    return lax.dot_general(
        left, right, (((1,), (1,)), ((), ())), preferred_element_type=jnp.float32
    )


def local(
    tokens,
    segments,
    w_qkv,
    b_qkv,
    w_out,
    b_out,
    norm_gain,
    norm_bias,
    w_up,
    b_up,
    w_down,
    b_down,
    prefix,
    cotangent,
):
    seqs_here, tok_here, model_width = tokens.shape
    rows_here = seqs_here * tok_here
    head_count = HEADS
    head_size = model_width // head_count
    score_scale = 1.0 / math.sqrt(head_size)
    rim_rows = PAIR_MAX
    prefix_len = prefix.shape[2]
    position = lax.axis_index("wide") * tok_here
    padded_ids = jnp.pad(segments, ((0, 0), (rim_rows, rim_rows)), constant_values=-1)
    query_ids = lax.dynamic_slice_in_dim(segments, position, tok_here, 1)
    window_ids = lax.dynamic_slice_in_dim(padded_ids, position, tok_here + 2 * rim_rows, 1)
    prefix_mask = jnp.ones((seqs_here, prefix_len, tok_here), dtype=bool)
    visible = jnp.concatenate(
        [prefix_mask, window_ids[:, :, None] == query_ids[:, None, :]], axis=1
    )[:, None]

    def split_heads(values):
        return values.reshape(seqs_here, values.shape[1], head_count, head_size)

    def with_prefix(layer_index, member, window_part):
        fixed_rows = jnp.broadcast_to(
            prefix[layer_index, member][None], (seqs_here, prefix_len, model_width)
        )
        return split_heads(jnp.concatenate([fixed_rows, window_part], axis=1))

    def score_block(queries, key_all):
        scores = (
            jnp.einsum("sqhe,skhe->shkq", queries, key_all, preferred_element_type=jnp.float32)
            * score_scale
        )
        return jnp.where(visible, scores, -1e30)

    hidden = tokens.astype(jnp.float32).reshape(rows_here, model_width)
    stored = []
    for layer_index in range(LAYERS):
        qkv_all = multiply(hidden.astype(jnp.bfloat16), w_qkv[layer_index]) + b_qkv[layer_index]
        qkv_low = qkv_all.astype(jnp.bfloat16).reshape(seqs_here, tok_here, 3 * model_width)
        queries = split_heads(qkv_low[:, :, :model_width])
        window = extended(qkv_low[:, :, model_width:], (("wide", 1),), rim_rows)
        key_all = with_prefix(layer_index, 0, window[:, :, :model_width])
        value_all = with_prefix(layer_index, 1, window[:, :, model_width:])
        scores = score_block(queries, key_all)
        top_score = jnp.max(scores, axis=2, keepdims=True)
        exp_scores = jnp.exp(scores - top_score)
        denominator = jnp.sum(exp_scores, axis=2, keepdims=True)
        probs_low = (exp_scores / denominator).astype(jnp.bfloat16)
        log_total = top_score + jnp.log(denominator)
        context = jnp.einsum(
            "shkq,skhe->sqhe", probs_low, value_all, preferred_element_type=jnp.float32
        )
        context_low = context.astype(jnp.bfloat16).reshape(rows_here, model_width)
        attention = multiply(context_low, w_out[layer_index]) + b_out[layer_index]
        pre_norm = hidden + attention
        normed = normalize(pre_norm, norm_gain[layer_index, 0], norm_bias[layer_index, 0])
        normed_low = normed.astype(jnp.bfloat16)
        up_rows = lax.all_gather(w_up[layer_index], "wide", axis=0, tiled=True)
        down_rows = lax.all_gather(w_down[layer_index], "wide", axis=0, tiled=True)
        bias_rows = lax.all_gather(b_up[layer_index], "wide", axis=0, tiled=True)
        pre_rows = multiply_back(normed_low, up_rows) + bias_rows.astype(jnp.float32)
        ffn_out = multiply(gelu_exact(pre_rows).astype(jnp.bfloat16), down_rows)
        kept_ffn = ()
        second_in = normed + ffn_out + b_down[layer_index]
        stored.append(
            (queries, key_all, value_all, log_total, pre_norm, normed_low, second_in, kept_ffn)
        )
        hidden = normalize(second_in, norm_gain[layer_index, 1], norm_bias[layer_index, 1])
    output = hidden.astype(jnp.bfloat16).reshape(seqs_here, tok_here, model_width)
    grad_hidden = cotangent.astype(jnp.float32).reshape(rows_here, model_width)
    prefix_grads = [None] * LAYERS
    for layer_index in reversed(range(LAYERS)):
        queries, key_all, value_all, log_total, pre_norm, normed_low, second_in, kept_ffn = stored[
            layer_index
        ]
        grad_sum2 = norm_grad(
            second_in, norm_gain[layer_index, 1], norm_bias[layer_index, 1], grad_hidden
        )
        grad_ffn_low = grad_sum2.astype(jnp.bfloat16)
        back_up_rows = lax.all_gather(w_up[layer_index], "wide", axis=0, tiled=True)
        back_down_rows = lax.all_gather(w_down[layer_index], "wide", axis=0, tiled=True)
        back_bias_rows = lax.all_gather(b_up[layer_index], "wide", axis=0, tiled=True)
        back_pre_rows = multiply_back(normed_low, back_up_rows) + back_bias_rows.astype(jnp.float32)
        grad_rows = gelu_back(back_pre_rows, multiply_back(grad_ffn_low, back_down_rows)).astype(
            jnp.bfloat16
        )
        grad_from_ffn = multiply(grad_rows, back_up_rows)
        grad_normed = grad_sum2 + grad_from_ffn
        grad_sum1 = norm_grad(
            pre_norm, norm_gain[layer_index, 0], norm_bias[layer_index, 0], grad_normed
        )
        grad_attn_low = grad_sum1.astype(jnp.bfloat16)
        grad_context = multiply_back(grad_attn_low, w_out[layer_index]).astype(jnp.bfloat16)
        grad_context = split_heads(grad_context.reshape(seqs_here, tok_here, model_width))
        scores = score_block(queries, key_all)
        probs = jnp.exp(scores - log_total)
        probs_low = probs.astype(jnp.bfloat16)
        grad_probs = jnp.einsum(
            "sqhe,skhe->shkq", grad_context, value_all, preferred_element_type=jnp.float32
        )
        row_dot = jnp.sum(probs * grad_probs, axis=2, keepdims=True)
        grad_scores = (probs * (grad_probs - row_dot)).astype(jnp.bfloat16)
        grad_queries = (
            jnp.einsum("shkq,skhe->sqhe", grad_scores, key_all, preferred_element_type=jnp.float32)
            * score_scale
        )
        grad_keys = (
            jnp.einsum("shkq,sqhe->skhe", grad_scores, queries, preferred_element_type=jnp.float32)
            * score_scale
        )
        grad_values = jnp.einsum(
            "shkq,sqhe->skhe", probs_low, grad_context, preferred_element_type=jnp.float32
        )
        key_count = grad_keys.shape[1]
        grad_keys = grad_keys.reshape(seqs_here, key_count, model_width)
        grad_values = grad_values.reshape(seqs_here, key_count, model_width)
        prefix_grads[layer_index] = jnp.stack(
            [
                jnp.sum(grad_keys[:, :prefix_len], axis=0),
                jnp.sum(grad_values[:, :prefix_len], axis=0),
            ],
            axis=0,
        )
        grad_window = jnp.concatenate(
            [grad_keys[:, prefix_len:], grad_values[:, prefix_len:]], axis=2
        )
        grad_kv = grad_window[:, rim_rows : rim_rows + tok_here]
        rim_grads = jnp.concatenate(
            [grad_window[:, :rim_rows], grad_window[:, rim_rows + tok_here :]], axis=1
        )
        returned = extended(rim_grads.astype(jnp.bfloat16), (("wide", 1),), rim_rows).astype(
            rim_grads.dtype
        )
        grad_kv = grad_kv + returned[:, :rim_rows]
        grad_kv = grad_kv + returned[:, 3 * rim_rows :]
        grad_qkv = jnp.concatenate(
            [grad_queries.reshape(seqs_here, tok_here, model_width), grad_kv], axis=2
        )
        grad_qkv = grad_qkv.astype(jnp.bfloat16).reshape(rows_here, 3 * model_width)
        grad_hidden = grad_sum1 + multiply_back(grad_qkv, w_qkv[layer_index])
    grad_prefix = lax.psum(jnp.stack(prefix_grads, axis=0), ("rows", "wide"))
    return (output, grad_hidden.reshape(seqs_here, tok_here, model_width), grad_prefix)


def solution(mesh):
    return jax.shard_map(
        local,
        mesh=mesh,
        in_specs=(
            P("rows", "wide", None),
            P("rows", None),
            P(),
            P(),
            P(),
            P(),
            P(),
            P(),
            P(None, "wide", None),
            P(None, "wide"),
            P(None, "wide", None),
            P(),
            P(),
            P("rows", "wide", None),
        ),
        out_specs=(P("rows", "wide", None), P("rows", "wide", None), P()),
        check_vma=False,
    )
```

profile of v0, /device:TPU:0, one launch (start us, length us, event | category | flops | bytes accessed | tf_op | source)
XLA Modules:
  0.0 841.0 jit_solution(1946470250862313874)
XLA Ops:
  12.1 6.5 add_convert_fusion.3
  21.5 4.4 collective-permute-start
  28.2 91.8 %all-gather.1 = bf16[1,4096]{1,0:T(2,128)(2,1)S(1)} all-gather(bf16[1,512]{1,0:T(2,128)(2,1)S(1)} %get-tuple-element.50), channel_id=3, replica_groups=mesh['rows'=4,'wide'=8] {'wide'}, dimensions={1}, use_global_device_ids=true | all-gather | bytes 9216 | tf_op jit(solution)/shard_map/all_gather | solution.py:126
  134.3 6.1 copy.49
  140.4 6.7 copy.50
  147.1 10.5 %fusion.193 = (f32[4,16,128]{2,1,0:T(8,128)S(1)}, f32[4,16,448,128]{3,2,1,0:T(8,128)}) fusion(bf16[4,448,16,64]{1,3,2,0:T(8,128)(2,1)} %bitcast.215, bf16[4,128,16,64]{1,3,2,0:T(8,128)(2,1)S(1)} %bitcast.223, pred[4,448,128]{2,1,0:T(8,128)(4,1)S(1)} %concatenate.59), kind=kOutput, calls=%fused_computation.264 | convolution fusion | flops 480763904 | bytes 19660800 | tf_op jit(solution)/shard_map/sqhe,skhe->shkq/dot_general | solution.py:96
  157.6 9.0 %fusion = f32[4,16,128]{2,1,0:T(8,128)S(1)} fusion(f32[4,16,448,128]{3,2,1,0:T(8,128)} %get-tuple-element.52, f32[4,16,128]{2,1,0:T(8,128)S(1)} %get-tuple-element.51), kind=kLoop, calls=%fused_computation.18 | loop fusion | flops 7331840 | bytes 14745600 | tf_op jit(solution)/shard_map/reduce_sum | solution.py:113
  166.7 8.5 %fusion.134 = bf16[4,128,16,64]{1,3,2,0:T(8,128)(2,1)S(1)} fusion(bf16[4,448,16,64]{1,3,2,0:T(8,128)(2,1)S(1)} %bitcast.227, f32[4,16,448,128]{3,2,1,0:T(8,128)} %get-tuple-element.52, f32[4,16,128]{2,1,0:T(8,128)S(1)} %fusion, f32[4,16,128]{2,1,0:T(8,128)S(1)} %get-tuple-element.51), kind=kOutput, calls=%fused_computation.183 | convolution fusion | flops 481296384 | bytes 19464192 | tf_op jit(solution)/shard_map/shkq,skhe->sqhe/dot_general | solution.py:116
  178.0 27.0 %fusion.6 = (f32[512,4096]{1,0:T(8,128)}, f32[512,4096]{1,0:T(8,128)}) fusion(f32[4096]{0:T(1024)S(1)} %bitcast.247, bf16[1,4096,1024]{2,1,0:T(8,128)(2,1)} %all-gather.11.cloned.1.call-done, f32[512,1024]{1,0:T(8,128)S(1)} %get-tuple-element.54, f32[1024]{0:T(1024)} %bitcast.272, f32[1024]{0:T(1024)S(1)} %bitcast.259, f32[512]{0:T(512)S(1)} %fusion.163, ...), kind=kOutput, calls=%fused_computation.26 | convolution fusion | flops 4429709312 | bytes 27291648 | tf_op jit(solution)/shard_map/dot_general | solution.py:48
  205.0 12.3 %fusion.195 = (f32[512]{0:T(512)S(1)}, f32[512,1024]{1,0:T(8,128)S(1)}) fusion(f32[1024]{0:T(1024)S(1)} %bitcast.257, bf16[1,4096,1024]{2,1,0:T(8,128)(2,1)} %all-gather.13.cloned.1.call-done, f32[512,4096]{1,0:T(8,128)} %get-tuple-element.55, f32[512,4096]{1,0:T(8,128)} %get-tuple-element.56, f32[4096]{0:T(1024)S(1)} %bitcast.248, ...), kind=kOutput, calls=%fused_computation.266 | convolution fusion | flops 4307025408 | bytes 29394944 | tf_op jit(solution)/shard_map/dot_general | solution.py:44
  217.7 7.1 add_convert_fusion.2
  227.7 4.4 collective-permute-start.2
  232.2 74.9 %all-gather.4 = bf16[1,4096]{1,0:T(2,128)(2,1)S(1)} all-gather(bf16[1,512]{1,0:T(2,128)(2,1)S(1)} %get-tuple-element.49), channel_id=6, replica_groups=mesh['rows'=4,'wide'=8] {'wide'}, dimensions={1}, use_global_device_ids=true | all-gather | bytes 9216 | tf_op jit(solution)/shard_map/all_gather | solution.py:126
  319.5 6.1 copy.54
  325.7 4.1 pad_maximum_fusion.6
  329.9 6.3 copy.53
  336.2 10.6 %fusion.196 = (f32[4,16,128]{2,1,0:T(8,128)S(1)}, f32[4,16,448,128]{3,2,1,0:T(8,128)}) fusion(bf16[4,448,16,64]{1,3,2,0:T(8,128)(2,1)} %bitcast.217, bf16[4,128,16,64]{1,3,2,0:T(8,128)(2,1)S(1)} %bitcast.225, pred[4,448,128]{2,1,0:T(8,128)(4,1)S(1)} %concatenate.59), kind=kOutput, calls=%fused_computation.267 | convolution fusion | flops 480763904 | bytes 19660800 | tf_op jit(solution)/shard_map/sqhe,skhe->shkq/dot_general | solution.py:96
  346.8 9.1 %fusion.1 = f32[4,16,128]{2,1,0:T(8,128)S(1)} fusion(f32[4,16,448,128]{3,2,1,0:T(8,128)} %get-tuple-element.60, f32[4,16,128]{2,1,0:T(8,128)S(1)} %get-tuple-element.59), kind=kLoop, calls=%fused_computation.19 | loop fusion | flops 7331840 | bytes 14745600 | tf_op jit(solution)/shard_map/reduce_sum | solution.py:113
  355.9 8.6 %fusion.135 = bf16[4,128,16,64]{1,3,2,0:T(8,128)(2,1)S(1)} fusion(bf16[4,448,16,64]{1,3,2,0:T(8,128)(2,1)S(1)} %bitcast.229, f32[4,16,448,128]{3,2,1,0:T(8,128)} %get-tuple-element.60, f32[4,16,128]{2,1,0:T(8,128)S(1)} %fusion.1, f32[4,16,128]{2,1,0:T(8,128)S(1)} %get-tuple-element.59), kind=kOutput, calls=%fused_computation.184 | convolution fusion | flops 481296384 | bytes 19464192 | tf_op jit(solution)/shard_map/shkq,skhe->sqhe/dot_general | solution.py:116
  367.9 26.7 %fusion.7 = (f32[512,4096]{1,0:T(8,128)}, f32[512,4096]{1,0:T(8,128)}) fusion(f32[4096]{0:T(1024)S(1)} %bitcast.250, bf16[1,4096,1024]{2,1,0:T(8,128)(2,1)} %all-gather.15.cloned.1.call-done, f32[512,1024]{1,0:T(8,128)S(1)} %get-tuple-element.62, f32[1024]{0:T(1024)S(1)} %bitcast.268, f32[1024]{0:T(1024)S(1)} %bitcast.265, f32[512]{0:T(512)S(1)} %fusion.165, ...), kind=kOutput, calls=%fused_computation.27 | convolution fusion | flops 4429709312 | bytes 27291648 | tf_op jit(solution)/shard_map/dot_general | solution.py:48
  394.6 11.0 %fusion.198 = (f32[512]{0:T(512)S(1)}, f32[512,1024]{1,0:T(8,128)S(1)}) fusion(f32[1024]{0:T(1024)S(1)} %bitcast.255, bf16[1,4096,1024]{2,1,0:T(8,128)(2,1)} %all-gather.17.cloned.1.call-done, f32[512,4096]{1,0:T(8,128)} %get-tuple-element.63, f32[512,4096]{1,0:T(8,128)} %get-tuple-element.64, f32[4096]{0:T(1024)S(1)} %bitcast.251, ...), kind=kOutput, calls=%fused_computation.269 | convolution fusion | flops 4307025408 | bytes 29394944 | tf_op jit(solution)/shard_map/dot_general | solution.py:44
  408.8 23.4 %multiply_reduce_fusion.4 = (f32[512]{0:T(512)S(1)}, f32[512,1024]{1,0:T(8,128)}) fusion(f32[512,1024]{1,0:T(8,128)S(1)} %get-tuple-element.62, f32[512]{0:T(512)S(1)} %broadcast_multiply_fusion.3, f32[1024]{0:T(1024)S(1)} %bitcast.267, bf16[1,4096,1024]{2,1,0:T(8,128)(2,1)} %all-gather.15.cloned.1.call-done, f32[512,4096]{1,0:T(8,128)} %get-tuple-element.63, ...), kind=kOutput, calls=%fused_computation.153 | convolution fusion | flops 8625586176 | bytes 39872512 | tf_op jit(solution)/shard_map/dot_general | solution.py:44
  440.4 12.0 %fusion.36 = f32[4,16,64,448]{3,2,1,0:T(8,128)} fusion(bf16[4,128,16,64]{1,3,2,0:T(8,128)(2,1)S(1)} %copy.58, f32[4,16,448,128]{3,2,1,0:T(8,128)} %get-tuple-element.60, f32[4,16,128]{2,1,0:T(8,128)S(1)} %log_add_fusion.1), kind=kOutput, calls=%fused_computation.75 | convolution fusion | flops 477102080 | bytes 23101440 | tf_op jit(solution)/shard_map/shkq,sqhe->skhe/dot_general | solution.py:177
  452.4 10.4 %multiply_reduce_fusion.1 = (f32[4,16,128]{2,1,0:T(8,128)S(1)}, f32[4,16,448,128]{3,2,1,0:T(8,128)}) fusion(f32[4,16,448,128]{3,2,1,0:T(8,128)} %get-tuple-element.60, f32[4,16,128]{2,1,0:T(8,128)S(1)} %log_add_fusion.1, bf16[4,448,16,64]{1,3,2,0:T(8,128)(2,1)S(1)} %bitcast.230, bf16[4,128,16,64]{1,3,2,0:T(8,128)(2,1)S(1)} %copy.58), kind=kOutput, calls=%fused_computation.10 | convolution fusion | flops 480763904 | bytes 34144256 | tf_op jit(solution)/shard_map/sqhe,skhe->shkq/dot_general | solution.py:164
  462.8 7.9 slice.247
  470.6 6.6 copy.81
  477.2 10.5 %multiply_convert_fusion.1 = bf16[4,16,448,128]{3,2,1,0:T(8,128)(2,1)S(1)} fusion(f32[4,16,448,128]{3,2,1,0:T(8,128)} %get-tuple-element.70, f32[4,16,448,128]{3,2,1,0:T(8,128)} %get-tuple-element.60, f32[4,16,128]{2,1,0:T(8,128)S(1)} %get-tuple-element.69, f32[4,16,128]{2,1,0:T(8,128)S(1)} %log_add_fusion.1), kind=kLoop, calls=%fused_computation.9 | loop fusion | flops 14680064 | bytes 36765696 | tf_op jit(solution)/shard_map/convert_element_type | solution.py:168
  494.3 4.3 slice.246
  498.6 6.6 copy.80
  505.2 8.2 fusion.3
  513.4 4.9 fusion.182
  523.2 4.8 fusion.136
  531.6 4.1 fusion.61
  536.3 6.6 multiply_reduce_fusion.3
  544.9 23.6 %multiply_reduce_fusion.2 = (f32[512]{0:T(512)S(1)}, f32[512,1024]{1,0:T(8,128)}) fusion(f32[512,1024]{1,0:T(8,128)S(1)} %copy-done.14, f32[512]{0:T(512)S(1)} %copy-done.35, f32[1024]{0:T(1024)S(1)} %bitcast.261, bf16[1,4096,1024]{2,1,0:T(8,128)(2,1)} %all-gather.11.cloned.1.call-done, f32[512,4096]{1,0:T(8,128)} %get-tuple-element.55, ...), kind=kOutput, calls=%fused_computation.148 | convolution fusion | flops 8625586176 | bytes 39872512 | tf_op jit(solution)/shard_map/dot_general | solution.py:44
  576.6 11.8 %fusion.34 = f32[4,16,64,448]{3,2,1,0:T(8,128)} fusion(bf16[4,128,16,64]{1,3,2,0:T(8,128)(2,1)S(1)} %copy.65, f32[4,16,448,128]{3,2,1,0:T(8,128)} %get-tuple-element.52, f32[4,16,128]{2,1,0:T(8,128)S(1)} %log_add_fusion), kind=kOutput, calls=%fused_computation.74 | convolution fusion | flops 477102080 | bytes 23101440 | tf_op jit(solution)/shard_map/shkq,sqhe->skhe/dot_general | solution.py:177
  588.5 10.1 %multiply_reduce_fusion = (f32[4,16,128]{2,1,0:T(8,128)S(1)}, f32[4,16,448,128]{3,2,1,0:T(8,128)}) fusion(f32[4,16,448,128]{3,2,1,0:T(8,128)} %get-tuple-element.52, f32[4,16,128]{2,1,0:T(8,128)S(1)} %log_add_fusion, bf16[4,448,16,64]{1,3,2,0:T(8,128)(2,1)S(1)} %bitcast.228, bf16[4,128,16,64]{1,3,2,0:T(8,128)(2,1)S(1)} %copy.65), kind=kOutput, calls=%fused_computation.7 | convolution fusion | flops 480763904 | bytes 34144256 | tf_op jit(solution)/shard_map/sqhe,skhe->shkq/dot_general | solution.py:164
  598.6 7.7 slice.253
  606.3 6.6 copy.83
  612.9 10.7 %multiply_convert_fusion = bf16[4,16,448,128]{3,2,1,0:T(8,128)(2,1)S(1)} fusion(f32[4,16,448,128]{3,2,1,0:T(8,128)} %get-tuple-element.76, f32[4,16,448,128]{3,2,1,0:T(8,128)} %get-tuple-element.52, f32[4,16,128]{2,1,0:T(8,128)S(1)} %get-tuple-element.75, f32[4,16,128]{2,1,0:T(8,128)S(1)} %log_add_fusion), kind=kLoop, calls=%fused_computation.6 | loop fusion | flops 14680064 | bytes 36765696 | tf_op jit(solution)/shard_map/convert_element_type | solution.py:168
  630.1 4.3 slice.252
  634.4 6.6 copy.82
  641.0 8.2 fusion.2
  649.3 4.9 fusion.181
  654.1 19.9 %collective-permute-start.6 = (bf16[4,128,2048]{2,1,0:T(8,128)(2,1)}, bf16[4,128,2048]{2,1,0:T(8,128)(2,1)}, u32[]{:S(2)}, u32[]{:S(2)}) collective-permute-start(bf16[4,128,2048]{2,1,0:T(8,128)(2,1)} %get-tuple-element.16), channel_id=1, source_target_pairs={{0,1},{1,2},{2,3},{3,4},{4,5},{5,6},{6,7},{8,9},{9,10},{10,11},{11... | collective-permute-start | bytes 6291464 | tf_op jit(solution)/shard_map/ppermute | solution.py:17
  684.1 6.0 fusion.137
  693.5 125.9 %all-reduce.4.cloned.1.call-done = f32[2,2,64,1024]{2,3,1,0:T(8,128)} async-done(((f32[2,2,64,1024]{2,3,1,0:T(8,128)}), f32[2,2,64,1024]{2,3,1,0:T(8,128)}) %all-reduce.4.cloned.1.call-update) | async-done | bytes 1048592 | tf_op jit(solution)/shard_map/psum | solution.py:207
  826.6 7.5 add_add_fusion.8
  (248 shorter events, 110.0 us)
Async XLA Ops:
  7.2 170.8 %all-gather.11.cloned.1.call-start = ((), (), s32[]{:S(2)}) async-start(), calls=%async_computation.1 | async-start | bytes 9437184 | tf_op jit(solution)/shard_map/all_gather | solution.py:124
  10.4 194.5 %all-gather.13.cloned.1.call-start = ((), (), s32[]{:S(2)}) async-start(), calls=%async_computation.2 | async-start | bytes 9437184 | tf_op jit(solution)/shard_map/all_gather | solution.py:125
  12.0 355.8 %all-gather.15.cloned.1.call-start = ((), (), s32[]{:S(2)}) async-start(), calls=%async_computation.3 | async-start | bytes 9437184 | tf_op jit(solution)/shard_map/all_gather | solution.py:124
  18.6 9.6 %copy-start.53 = (bf16[2,512]{1,0:T(2,128)(2,1)S(1)}, bf16[2,512]{1,0:T(2,128)(2,1)}, u32[]{:S(2)}) copy-start(bf16[2,512]{1,0:T(2,128)(2,1)} %param.23) | copy-start | bytes 6148
  18.6 103.1 %copy-start.33 = (s32[4,1024]{1,0:T(4,128)S(1)}, s32[4,1024]{1,0:T(4,128)}, u32[]{:S(2)}) copy-start(s32[4,1024]{1,0:T(4,128)} %param.15) | copy-start | bytes 49156
  18.6 103.4 %copy-start.51 = (f32[2,1024]{1,0:T(2,128)S(1)}, f32[2,1024]{1,0:T(2,128)}, u32[]{:S(2)}) copy-start(f32[2,1024]{1,0:T(2,128)} %param.19) | copy-start | bytes 24580
  18.6 104.0 %copy-start.52 = (f32[2,1024]{1,0:T(2,128)S(1)}, f32[2,1024]{1,0:T(2,128)}, u32[]{:S(2)}) copy-start(f32[2,1024]{1,0:T(2,128)} %param.25) | copy-start | bytes 24580
  18.6 104.6 %copy-start.43 = (f32[2,2,1024]{2,1,0:T(2,128)S(1)}, f32[2,2,1024]{2,1,0:T(2,128)}, u32[]{:S(2)}) copy-start(f32[2,2,1024]{2,1,0:T(2,128)} %param.20) | copy-start | bytes 49156
  18.6 105.2 %copy-start.44 = (f32[2,2,1024]{2,1,0:T(2,128)S(1)}, f32[2,2,1024]{2,1,0:T(2,128)}, u32[]{:S(2)}) copy-start(f32[2,2,1024]{2,1,0:T(2,128)} %param.21) | copy-start | bytes 49156
  20.2 106.2 %collective-permute-start.1 = (bf16[4,128,2048]{2,1,0:T(8,128)(2,1)S(1)}, bf16[4,128,2048]{2,1,0:T(8,128)(2,1)}, u32[]{:S(2)}, u32[]{:S(2)}) collective-permute-start(bf16[4,128,2048]{2,1,0:T(8,128)(2,1)S(1)} %slice.238), channel_id=1, source_target_pairs={{1,0},{2,1},{3,2},{4,3},{5,4},{6,5},{7,6},{9,8},{10,9},{11,10},{12... | collective-permute-start | bytes 6291464 | tf_op jit(solution)/shard_map/ppermute | solution.py:20
  21.5 104.9 %collective-permute-start = (bf16[4,128,2048]{2,1,0:T(8,128)(2,1)S(1)}, bf16[4,128,2048]{2,1,0:T(8,128)(2,1)}, u32[]{:S(2)}, u32[]{:S(2)}) collective-permute-start(bf16[4,128,2048]{2,1,0:T(8,128)(2,1)S(1)} %slice.238), channel_id=1, source_target_pairs={{0,1},{1,2},{2,3},{3,4},{4,5},{5,6},{6,7},{8,9},{9,10},{10,11},{11... | collective-permute-start | bytes 6291464 | tf_op jit(solution)/shard_map/ppermute | solution.py:17
  25.9 368.6 %all-gather.17.cloned.1.call-start = ((), (), s32[]{:S(2)}) async-start(), calls=%async_computation.4 | async-start | bytes 9437184 | tf_op jit(solution)/shard_map/all_gather | solution.py:125
  120.0 84.9 %copy-start.45 = (f32[1,4096]{1,0:T(1,128)}, f32[1,4096]{1,0:T(1,128)S(1)}, u32[]{:S(2)}) copy-start(f32[1,4096]{1,0:T(1,128)S(1)} %convert_element_type.132) | copy-start | bytes 49156
  121.7 25.4 %copy-start.5 = (bf16[4,128,1024]{1,2,0:T(8,128)(2,1)}, bf16[4,128,1024]{1,2,0:T(8,128)(2,1)S(1)}, u32[]{:S(2)}) copy-start(bf16[4,128,1024]{1,2,0:T(8,128)(2,1)S(1)} %copy.51) | copy-start | bytes 3145732
  123.8 81.1 %copy-start.56 = (f32[1,1,1024]{2,1,0:T(1,128)}, f32[1,1,1024]{2,1,0:T(1,128)S(1)}, u32[]{:S(2)}) copy-start(f32[1,1,1024]{2,1,0:T(1,128)S(1)} %get-tuple-element.37) | copy-start | bytes 12292
  123.8 241.5 %copy-start.58 = (f32[1,1,1024]{2,1,0:T(1,128)}, f32[1,1,1024]{2,1,0:T(1,128)S(1)}, u32[]{:S(2)}) copy-start(f32[1,1,1024]{2,1,0:T(1,128)S(1)} %get-tuple-element.36) | copy-start | bytes 12292
  177.5 27.4 %copy-start.13 = (f32[512,1024]{1,0:T(8,128)}, f32[512,1024]{1,0:T(8,128)S(1)}, u32[]{:S(2)}) copy-start(f32[512,1024]{1,0:T(8,128)S(1)} %get-tuple-element.54) | copy-start | bytes 6291460
  177.6 27.4 %copy-start.34 = (f32[512]{0:T(512)}, f32[512]{0:T(512)S(1)}, u32[]{:S(2)}) copy-start(f32[512]{0:T(512)S(1)} %broadcast_multiply_fusion.5) | copy-start | bytes 6148
  177.9 27.0 %copy-start.38 = (f32[512]{0:T(512)}, f32[512]{0:T(512)S(1)}, u32[]{:S(2)}) copy-start(f32[512]{0:T(512)S(1)} %multiply_reduce_fusion.8) | copy-start | bytes 6148
  177.9 27.1 %copy-start.47 = (f32[512]{0:T(512)}, f32[512]{0:T(512)S(1)}, u32[]{:S(2)}) copy-start(f32[512]{0:T(512)S(1)} %fusion.163) | copy-start | bytes 6148
  178.0 27.0 %copy-start.63 = (f32[1,1,1024]{2,1,0:T(1,128)S(1)}, f32[1,1,1024]{2,1,0:T(1,128)}, u32[]{:S(2)}) copy-start(f32[1,1,1024]{2,1,0:T(1,128)} %get-tuple-element.41) | copy-start | bytes 12292
  205.0 12.7 %copy-start.62 = (f32[1,1,1024]{2,1,0:T(1,128)S(1)}, f32[1,1,1024]{2,1,0:T(1,128)}, u32[]{:S(2)}) copy-start(f32[1,1,1024]{2,1,0:T(1,128)} %get-tuple-element.40) | copy-start | bytes 12292
  217.3 148.0 %copy-start.36 = (f32[512]{0:T(512)}, f32[512]{0:T(512)S(1)}, u32[]{:S(2)}) copy-start(f32[512]{0:T(512)S(1)} %broadcast_multiply_fusion.4) | copy-start | bytes 6148
  217.7 147.6 %copy-start.49 = (f32[512]{0:T(512)}, f32[512]{0:T(512)S(1)}, u32[]{:S(2)}) copy-start(f32[512]{0:T(512)S(1)} %fusion.164) | copy-start | bytes 6148
  226.4 84.6 %collective-permute-start.3 = (bf16[4,128,2048]{2,1,0:T(8,128)(2,1)S(1)}, bf16[4,128,2048]{2,1,0:T(8,128)(2,1)}, u32[]{:S(2)}, u32[]{:S(2)}) collective-permute-start(bf16[4,128,2048]{2,1,0:T(8,128)(2,1)S(1)} %slice.242), channel_id=1, source_target_pairs={{1,0},{2,1},{3,2},{4,3},{5,4},{6,5},{7,6},{9,8},{10,9},{11,10},{12... | collective-permute-start | bytes 6291464 | tf_op jit(solution)/shard_map/ppermute | solution.py:20
  227.7 83.3 %collective-permute-start.2 = (bf16[4,128,2048]{2,1,0:T(8,128)(2,1)S(1)}, bf16[4,128,2048]{2,1,0:T(8,128)(2,1)}, u32[]{:S(2)}, u32[]{:S(2)}) collective-permute-start(bf16[4,128,2048]{2,1,0:T(8,128)(2,1)S(1)} %slice.242), channel_id=1, source_target_pairs={{0,1},{1,2},{2,3},{3,4},{4,5},{5,6},{6,7},{8,9},{9,10},{10,11},{11... | collective-permute-start | bytes 6291464 | tf_op jit(solution)/shard_map/ppermute | solution.py:17
  232.1 587.3 %all-reduce.4.cloned.1.call-start = ((), (), s32[]{:S(2)}) async-start(), calls=%async_computation | async-start | bytes 4194304 | tf_op jit(solution)/shard_map/psum | solution.py:207
  311.0 25.2 %copy-start.7 = (bf16[4,128,1024]{1,2,0:T(8,128)(2,1)}, bf16[4,128,1024]{1,2,0:T(8,128)(2,1)S(1)}, u32[]{:S(2)}) copy-start(bf16[4,128,1024]{1,2,0:T(8,128)(2,1)S(1)} %copy.55) | copy-start | bytes 3145732
  355.8 9.5 %copy-start.16 = (f32[512,1024]{1,0:T(8,128)S(1)}, f32[512,1024]{1,0:T(8,128)}, u32[]{:S(2)}) copy-start(f32[512,1024]{1,0:T(8,128)} %copy-done.15) | copy-start | bytes 6291460
  355.8 9.5 %copy-start.55 = (f32[1,1024]{1,0:T(1,128)S(1)}, f32[1,1024]{1,0:T(1,128)}, u32[]{:S(2)}) copy-start(f32[1,1024]{1,0:T(1,128)} %get-tuple-element.45) | copy-start | bytes 12292
  355.8 9.5 %copy-start.65 = (bf16[2,1024,1024]{2,1,0:T(8,128)(2,1)S(1)}, bf16[2,1024,1024]{2,1,0:T(8,128)(2,1)}, u32[]{:S(2)}) copy-start(bf16[2,1024,1024]{2,1,0:T(8,128)(2,1)} %param.18) | copy-start | bytes 12582916
  367.9 26.7 %copy-start.54 = (f32[1,1024]{1,0:T(1,128)S(1)}, f32[1,1024]{1,0:T(1,128)}, u32[]{:S(2)}) copy-start(f32[1,1024]{1,0:T(1,128)} %get-tuple-element.43) | copy-start | bytes 12292
  394.5 11.0 %copy-start.18 = (bf16[4,128,1024]{2,1,0:T(8,128)(2,1)S(1)}, bf16[4,128,1024]{2,1,0:T(8,128)(2,1)}, u32[]{:S(2)}) copy-start(bf16[4,128,1024]{2,1,0:T(8,128)(2,1)} %param.27) | copy-start | bytes 3145732
  394.5 11.0 %copy-start.31 = (f32[1,1,1024]{2,1,0:T(1,128)S(1)}, f32[1,1,1024]{2,1,0:T(1,128)}, u32[]{:S(2)}) copy-start(f32[1,1,1024]{2,1,0:T(1,128)} %get-tuple-element.35) | copy-start | bytes 12292
  394.5 11.7 %copy-start.42 = (f32[1,1,1024]{2,1,0:T(1,128)S(1)}, f32[1,1,1024]{2,1,0:T(1,128)}, u32[]{:S(2)}) copy-start(f32[1,1,1024]{2,1,0:T(1,128)} %get-tuple-element.39) | copy-start | bytes 12292
  440.4 12.0 %copy-start.12 = (bf16[4,448,1024]{1,2,0:T(8,128)(2,1)S(1)}, bf16[4,448,1024]{1,2,0:T(8,128)(2,1)}, u32[]{:S(2)}) copy-start(bf16[4,448,1024]{1,2,0:T(8,128)(2,1)} %copy.53) | copy-start | bytes 11010052
  477.2 10.5 %copy-start.8 = (bf16[4,128,1024]{1,2,0:T(8,128)(2,1)S(1)}, bf16[4,128,1024]{1,2,0:T(8,128)(2,1)}, u32[]{:S(2)}) copy-start(bf16[4,128,1024]{1,2,0:T(8,128)(2,1)} %copy-done.7) | copy-start | bytes 3145732
  513.4 9.7 %copy-start.28 = (f32[4,16,128]{2,1,0:T(8,128)S(1)}, f32[4,16,128]{2,1,0:T(8,128)}, u32[]{:S(2)}) copy-start(f32[4,16,128]{2,1,0:T(8,128)} %copy-done.27) | copy-start | bytes 98308
  513.4 9.7 %copy-start.30 = (f32[4,16,128]{2,1,0:T(8,128)S(1)}, f32[4,16,128]{2,1,0:T(8,128)}, u32[]{:S(2)}) copy-start(f32[4,16,128]{2,1,0:T(8,128)} %copy-done.29) | copy-start | bytes 98308
  513.4 9.7 %copy-start.4 = (bf16[4,448,1024]{1,2,0:T(8,128)(2,1)S(1)}, bf16[4,448,1024]{1,2,0:T(8,128)(2,1)}, u32[]{:S(2)}) copy-start(bf16[4,448,1024]{1,2,0:T(8,128)(2,1)} %copy.54) | copy-start | bytes 11010052
  518.4 13.3 %collective-permute-start.4 = (bf16[4,128,2048]{2,1,0:T(8,128)(2,1)}, bf16[4,128,2048]{2,1,0:T(8,128)(2,1)}, u32[]{:S(2)}, u32[]{:S(2)}) collective-permute-start(bf16[4,128,2048]{2,1,0:T(8,128)(2,1)} %get-tuple-element.18), channel_id=1, source_target_pairs={{0,1},{1,2},{2,3},{3,4},{4,5},{5,6},{6,7},{8,9},{9,10},{10,11},{11... | collective-permute-start | bytes 6291464 | tf_op jit(solution)/shard_map/ppermute | solution.py:17
  521.8 9.8 %collective-permute-start.5 = (bf16[4,128,2048]{2,1,0:T(8,128)(2,1)}, bf16[4,128,2048]{2,1,0:T(8,128)(2,1)}, u32[]{:S(2)}, u32[]{:S(2)}) collective-permute-start(bf16[4,128,2048]{2,1,0:T(8,128)(2,1)} %get-tuple-element.19), channel_id=1, source_target_pairs={{1,0},{2,1},{3,2},{4,3},{5,4},{6,5},{7,6},{9,8},{10,9},{11,10},{12... | collective-permute-start | bytes 6291464 | tf_op jit(solution)/shard_map/ppermute | solution.py:20
  544.9 23.7 %copy-start.39 = (f32[512]{0:T(512)S(1)}, f32[512]{0:T(512)}, u32[]{:S(2)}) copy-start(f32[512]{0:T(512)} %copy-done.38) | copy-start | bytes 6148
  544.9 23.7 %copy-start.48 = (f32[512]{0:T(512)S(1)}, f32[512]{0:T(512)}, u32[]{:S(2)}) copy-start(f32[512]{0:T(512)} %copy-done.47) | copy-start | bytes 6148
  576.6 11.8 %copy-start.10 = (bf16[4,448,1024]{1,2,0:T(8,128)(2,1)S(1)}, bf16[4,448,1024]{1,2,0:T(8,128)(2,1)}, u32[]{:S(2)}) copy-start(bf16[4,448,1024]{1,2,0:T(8,128)(2,1)} %copy.49) | copy-start | bytes 11010052
  612.9 10.7 %copy-start.6 = (bf16[4,128,1024]{1,2,0:T(8,128)(2,1)S(1)}, bf16[4,128,1024]{1,2,0:T(8,128)(2,1)}, u32[]{:S(2)}) copy-start(bf16[4,128,1024]{1,2,0:T(8,128)(2,1)} %copy-done.5) | copy-start | bytes 3145732
  654.1 168.4 %collective-permute-start.6 = (bf16[4,128,2048]{2,1,0:T(8,128)(2,1)}, bf16[4,128,2048]{2,1,0:T(8,128)(2,1)}, u32[]{:S(2)}, u32[]{:S(2)}) collective-permute-start(bf16[4,128,2048]{2,1,0:T(8,128)(2,1)} %get-tuple-element.16), channel_id=1, source_target_pairs={{0,1},{1,2},{2,3},{3,4},{4,5},{5,6},{6,7},{8,9},{9,10},{10,11},{11... | collective-permute-start | bytes 6291464 | tf_op jit(solution)/shard_map/ppermute | solution.py:17
  674.0 148.6 %collective-permute-start.7 = (bf16[4,128,2048]{2,1,0:T(8,128)(2,1)}, bf16[4,128,2048]{2,1,0:T(8,128)(2,1)}, u32[]{:S(2)}, u32[]{:S(2)}) collective-permute-start(bf16[4,128,2048]{2,1,0:T(8,128)(2,1)} %get-tuple-element.17), channel_id=1, source_target_pairs={{1,0},{2,1},{3,2},{4,3},{5,4},{6,5},{7,6},{9,8},{10,9},{11,10},{12... | collective-permute-start | bytes 6291464 | tf_op jit(solution)/shard_map/ppermute | solution.py:20
  (35 other events, 159.4 us)
Sparse Core Ops, SparseCore 0:
  10.6 101.7 all-gather.10
  114.6 85.6 all-gather.12
  201.9 97.0 all-gather.14
  301.0 86.1 all-gather.16
  684.2 135.1 all-reduce.3
where the time goes:
time: 847 us; the launch traced here: 841 us
  matrix products  257 us (30%)
  blocking collectives  167 us (20%)
  local copies, waits for them, and re-layouts  137 us (16%)
  waiting for transfers between devices  126 us (15%)
  other arithmetic  101 us (12%)
  starting transfers between devices  37.4 us (4%)
  between operations  15.4 us (2%)
    all_gather x2, blocking collectives, local(): bias_rows = lax.all_gather(b_up[layer_index], 'wide', axis=0, tiled=True)  167 us
    psum x1, waiting for transfers between devices, local(): grad_prefix = lax.psum(jnp.stack(prefix_grads, axis=0), ('rows', 'wide'))  126 us
    dot_general x8, matrix products, multiply(): return jnp.dot(left, right, preferred_element_type=jnp.float32)  86.8 us
    dot_general x6, matrix products, multiply_back(): lax.dot_general(left, right, (((1,), (1,)), ((), ())), preferred_element_...  70.4 us
    unnamed x145, local copies, waits for them, and re-layouts  42.3 us
    ppermute x4, starting transfers between devices, extended(): lax.ppermute(lax.slice_in_dim(block, block.shape[dim] - width, None, axis...  32.1 us
    concatenate x4, local copies, waits for them, and re-layouts, with_prefix(): return split_heads(jnp.concatenate([fixed_rows, window_part], axis=1))  25.2 us
    another operation x4, other arithmetic  24.5 us
  transfers between devices with their start and end apart: 13, of which 1 were waited for; matrix products, arithmetic and copies ran while one was open for 28% of the time, Pallas kernels for 0%

commit v1 on v0

--- a/solution.py
+++ b/solution.py
@@ -7,6 +7,12 @@
 HEADS = 16
 PAIR_MAX = 128
 LAYERS = 2
+
+
+def joined_along(blocks, dim):
+    blocks = jnp.moveaxis(blocks, 0, dim)
+    shape = blocks.shape
+    return blocks.reshape(*shape[:dim], shape[dim] * shape[dim + 1], *shape[dim + 2 :])
 
 
 def extended(block, sides, width):
@@ -123,7 +129,19 @@
         normed_low = normed.astype(jnp.bfloat16)
         up_rows = lax.all_gather(w_up[layer_index], "wide", axis=0, tiled=True)
         down_rows = lax.all_gather(w_down[layer_index], "wide", axis=0, tiled=True)
-        bias_rows = lax.all_gather(b_up[layer_index], "wide", axis=0, tiled=True)
+        size = lax.axis_size("wide")
+        pairs = [(i_2, (i_2 + 1) % size) for i_2 in range(size)]
+        back = [(b, a) for a, b in pairs]
+        lower, upper = ([], [])
+        for step in range(size - 1):
+            if step % 2 == 0:
+                lower.append(lax.ppermute(lower[-1] if lower else b_up[layer_index], "wide", pairs))
+            else:
+                upper.append(lax.ppermute(upper[-1] if upper else b_up[layer_index], "wide", back))
+        blocks = jnp.stack([*lower[::-1], b_up[layer_index], *upper])
+        shift_2 = lax.axis_index("wide") - len(lower)
+        blocks = blocks[(jnp.arange(size) - shift_2) % size]
+        bias_rows = joined_along(blocks, 0)
         pre_rows = multiply_back(normed_low, up_rows) + bias_rows.astype(jnp.float32)
         ffn_out = multiply(gelu_exact(pre_rows).astype(jnp.bfloat16), down_rows)
         kept_ffn = ()

time: 847 us -> 911 us (1.076)
  starting transfers between devices: 37.4 us -> 161 us
  blocking collectives: 167 us -> 50.6 us
  matrix products: 257 us -> 298 us
    ppermute x0 -> x14, starting transfers between devices: none -> 140 us  [the longest x8 127 us: local(): lax.ppermute(lower[-1] if lower else b_up[layer_index], 'wide', pairs)]
    all_gather x2, blocking collectives: 167 us -> 50.6 us  [local(): lax.all_gather(b_up[layer_index], 'wide', axis=0, tiled=True)]
    dot_general x8, matrix products: 86.8 us -> 144 us  [multiply(): return jnp.dot(left, right, preferred_element_type=jnp.float32)]
    ppermute x4, starting transfers between devices: 32.1 us -> 16 us  [extended(): lax.ppermute(lax.slice_in_dim(block, block.shape[dim] - width, None, axis...]
    dot_general x6, matrix products: 70.4 us -> 54.7 us  [multiply_back(): lax.dot_general(left, right, (((1,), (1,)), ((), ())), preferred_element_...]
    unnamed x145 -> x169, local copies, waits for them, and re-layouts: 42.3 us -> 44.9 us
  transfers between devices with their start and end apart: 13 -> 27, of which waited for: 1 -> 8; matrix products, arithmetic and copies ran while one was open for 28% -> 26% of each run, Pallas kernels for 0% -> 0%
where the time goes in v1:
time: 911 us; the launch traced here: 904 us
  matrix products  298 us (33%)
  starting transfers between devices  161 us (18%)
  local copies, waits for them, and re-layouts  146 us (16%)
  waiting for transfers between devices  130 us (14%)
  other arithmetic  103 us (11%)
  blocking collectives  50.6 us (6%)
  between operations  15.5 us (2%)
    dot_general x8, matrix products, multiply(): return jnp.dot(left, right, preferred_element_type=jnp.float32)  144 us
    ppermute x8, starting transfers between devices, local(): lax.ppermute(lower[-1] if lower else b_up[layer_index], 'wide', pairs)  127 us
    psum x1, waiting for transfers between devices, local(): grad_prefix = lax.psum(jnp.stack(prefix_grads, axis=0), ('rows', 'wide'))  123 us
    dot_general x6, matrix products, multiply_back(): lax.dot_general(left, right, (((1,), (1,)), ((), ())), preferred_element_...  54.7 us
    all_gather x2, blocking collectives, local(): lax.all_gather(b_up[layer_index], 'wide', axis=0, tiled=True)  50.6 us
    unnamed x169, local copies, waits for them, and re-layouts  44.9 us
    concatenate x4, local copies, waits for them, and re-layouts, with_prefix(): return split_heads(jnp.concatenate([fixed_rows, window_part], axis=1))  25.3 us
    another operation x4, other arithmetic  24.6 us
  transfers between devices with their start and end apart: 27, of which 8 were waited for; matrix products, arithmetic and copies ran while one was open for 26% of the time, Pallas kernels for 0%

profile of v1, /device:TPU:0, one launch (start us, length us, event | category | flops | bytes accessed | tf_op | source)
XLA Modules:
  0.0 904.0 jit_solution(5711904893388860645)
XLA Ops:
  15.0 6.5 add_convert_fusion.1
  24.4 4.4 collective-permute-start
  38.8 59.4 %collective-permute-start.3 = (bf16[512]{0:T(512)(128)(2,1)S(1)}, bf16[512]{0:T(512)(128)(2,1)S(1)}, u32[]{:S(2)}, u32[]{:S(2)}) collective-permute-start(bf16[512]{0:T(512)(128)(2,1)S(1)} %collective-permute-done.2), channel_id=1, source_target_pairs={{0,1},{1,2},{2,3},{3,4},{4,5},{5,6},{6,7},{7,0},{8,9},{9,10},{10,1... | collective-permute-start | bytes 3080 | tf_op jit(solution)/shard_map/ppermute | solution.py:138
  99.0 15.1 %collective-permute-start.4 = (bf16[512]{0:T(512)(128)(2,1)S(1)}, bf16[512]{0:T(512)(128)(2,1)S(1)}, u32[]{:S(2)}, u32[]{:S(2)}) collective-permute-start(bf16[512]{0:T(512)(128)(2,1)S(1)} %collective-permute-done.3), channel_id=1, source_target_pairs={{0,1},{1,2},{2,3},{3,4},{4,5},{5,6},{6,7},{7,0},{8,9},{9,10},{10,1... | collective-permute-start | bytes 3080 | tf_op jit(solution)/shard_map/ppermute | solution.py:138
  133.8 6.2 copy.49
  140.0 6.5 copy.50
  146.5 10.5 %fusion.410 = (f32[4,16,128]{2,1,0:T(8,128)S(1)}, f32[4,16,448,128]{3,2,1,0:T(8,128)}) fusion(bf16[4,448,16,64]{1,3,2,0:T(8,128)(2,1)} %bitcast.219, bf16[4,128,16,64]{1,3,2,0:T(8,128)(2,1)S(1)} %bitcast.227, pred[4,448,128]{2,1,0:T(8,128)(4,1)S(1)} %concatenate.59), kind=kOutput, calls=%fused_computation.494 | convolution fusion | flops 480763904 | bytes 19660800 | tf_op jit(solution)/shard_map/sqhe,skhe->shkq/dot_general | solution.py:102
  157.0 9.0 fusion
  166.1 8.5 fusion.236
  178.3 24.2 %fusion.36 = f32[512,4096]{1,0:T(8,128)} fusion(bf16[1,4096,1024]{2,1,0:T(8,128)(2,1)} %all-gather.11.cloned.1.call-done, f32[512,1024]{1,0:T(8,128)S(1)} %get-tuple-element.56, f32[1024]{0:T(1024)S(1)} %bitcast.274, f32[1024]{0:T(1024)S(1)} %bitcast.261, f32[512]{0:T(512)S(1)} %fusion.265, f32[512]{0:T(512)S(1)} %broadcast_multiply_fusion.5), kind=kOutput, calls=%fused_computation.60 | convolution fusion | flops 4297588736 | bytes 18886656 | tf_op jit(solution)/shard_map/dot_general | solution.py:54
  202.6 26.5 %fusion.412 = (f32[512]{0:T(512)S(1)}, f32[512,1024]{1,0:T(8,128)S(1)}) fusion(f32[1024]{0:T(1024)S(1)} %bitcast.259, bf16[1,4096,1024]{2,1,0:T(8,128)(2,1)} %all-gather.13.cloned.1.call-done, f32[512,4096]{1,0:T(8,128)} %fusion.36, f32[4096]{0:T(1024)S(1)} %bitcast.253, f32[1024]{0:T(1024)S(1)} %bitcast.275, f32[1024]{0:T(1024)S(1)} %bitcast.262, ...), kind=kOutput, calls=%fused_computation.496 | convolution fusion | flops 4437048832 | bytes 21006336 | tf_op jit(solution)/shard_map/dot_general | solution.py:50
  230.4 6.9 add_convert_fusion
  240.2 4.4 collective-permute-start.9
  249.4 50.1 %collective-permute-start.12 = (bf16[512]{0:T(512)(128)(2,1)S(1)}, bf16[512]{0:T(512)(128)(2,1)S(1)}, u32[]{:S(2)}, u32[]{:S(2)}) collective-permute-start(bf16[512]{0:T(512)(128)(2,1)S(1)} %collective-permute-done.11), channel_id=1, source_target_pairs={{0,1},{1,2},{2,3},{3,4},{4,5},{5,6},{6,7},{7,0},{8,9},{9,10},{10,1... | collective-permute-start | bytes 3080 | tf_op jit(solution)/shard_map/ppermute | solution.py:138
  305.7 15.1 %all-gather.4 = bf16[1,4096]{1,0:T(2,128)(2,1)S(1)} all-gather(bf16[1,512]{1,0:T(2,128)(2,1)S(1)} %copy-done.41), channel_id=6, replica_groups=mesh['rows'=4,'wide'=8] {'wide'}, dimensions={1}, use_global_device_ids=true | all-gather | bytes 9216 | tf_op jit(solution)/shard_map/all_gather | solution.py:166
  334.6 6.1 copy.54
  345.0 6.5 copy.53
  351.6 10.6 %fusion.413 = (f32[4,16,128]{2,1,0:T(8,128)S(1)}, f32[4,16,448,128]{3,2,1,0:T(8,128)}) fusion(bf16[4,448,16,64]{1,3,2,0:T(8,128)(2,1)} %bitcast.221, bf16[4,128,16,64]{1,3,2,0:T(8,128)(2,1)S(1)} %bitcast.229, pred[4,448,128]{2,1,0:T(8,128)(4,1)S(1)} %copy-done.20), kind=kOutput, calls=%fused_computation.497 | convolution fusion | flops 480763904 | bytes 19660800 | tf_op jit(solution)/shard_map/sqhe,skhe->shkq/dot_general | solution.py:102
  362.1 9.1 %fusion.1 = f32[4,16,128]{2,1,0:T(8,128)S(1)} fusion(f32[4,16,448,128]{3,2,1,0:T(8,128)} %get-tuple-element.60, f32[4,16,128]{2,1,0:T(8,128)S(1)} %get-tuple-element.59), kind=kLoop, calls=%fused_computation.21 | loop fusion | flops 7331840 | bytes 14745600 | tf_op jit(solution)/shard_map/reduce_sum | solution.py:119
  371.3 8.5 fusion.237
  384.0 10.4 %fusion.28 = f32[512,4096]{1,0:T(8,128)} fusion(bf16[1,4096,1024]{2,1,0:T(8,128)(2,1)} %all-gather.15.cloned.1.call-done, f32[512,1024]{1,0:T(8,128)S(1)} %get-tuple-element.62, f32[1024]{0:T(1024)S(1)} %bitcast.270, f32[1024]{0:T(1024)S(1)} %bitcast.267, f32[512]{0:T(512)S(1)} %fusion.267, f32[512]{0:T(512)S(1)} %broadcast_multiply_fusion.3), kind=kOutput, calls=%fused_computation.52 | convolution fusion | flops 4297588736 | bytes 18886656 | tf_op jit(solution)/shard_map/dot_general | solution.py:54
  394.3 26.6 %fusion.415 = (f32[512]{0:T(512)S(1)}, f32[512,1024]{1,0:T(8,128)S(1)}) fusion(f32[1024]{0:T(1024)S(1)} %bitcast.257, bf16[1,4096,1024]{2,1,0:T(8,128)(2,1)} %all-gather.17.cloned.1.call-done, f32[512,4096]{1,0:T(8,128)} %fusion.28, f32[4096]{0:T(1024)S(1)} %bitcast.252, f32[1024]{0:T(1024)S(1)} %bitcast.271, f32[1024]{0:T(1024)S(1)} %bitcast.268, ...), kind=kOutput, calls=%fused_computation.499 | convolution fusion | flops 4437048832 | bytes 21006336 | tf_op jit(solution)/shard_map/dot_general | solution.py:50
  424.3 37.3 %multiply_reduce_fusion.4 = (f32[512]{0:T(512)S(1)}, f32[512,1024]{1,0:T(8,128)}) fusion(f32[512,1024]{1,0:T(8,128)S(1)} %get-tuple-element.62, f32[512]{0:T(512)S(1)} %broadcast_multiply_fusion.3, f32[1024]{0:T(1024)S(1)} %bitcast.269, bf16[1,4096,1024]{2,1,0:T(8,128)(2,1)} %all-gather.15.cloned.1.call-done, f32[512,4096]{1,0:T(8,128)} %fusion.28, ...), kind=kOutput, calls=%fused_computation.259 | convolution fusion | flops 8747220992 | bytes 31483904 | tf_op jit(solution)/shard_map/dot_general | solution.py:50
  471.2 11.9 %fusion.68 = f32[4,16,64,448]{3,2,1,0:T(8,128)} fusion(bf16[4,128,16,64]{1,3,2,0:T(8,128)(2,1)S(1)} %copy.58, f32[4,16,448,128]{3,2,1,0:T(8,128)} %get-tuple-element.60, f32[4,16,128]{2,1,0:T(8,128)S(1)} %copy-done.31), kind=kOutput, calls=%fused_computation.123 | convolution fusion | flops 477102080 | bytes 23101440 | tf_op jit(solution)/shard_map/shkq,sqhe->skhe/dot_general | solution.py:195
  483.1 10.2 %multiply_reduce_fusion.1 = (f32[4,16,128]{2,1,0:T(8,128)S(1)}, f32[4,16,448,128]{3,2,1,0:T(8,128)}) fusion(f32[4,16,448,128]{3,2,1,0:T(8,128)} %get-tuple-element.60, f32[4,16,128]{2,1,0:T(8,128)S(1)} %copy-done.31, bf16[4,448,16,64]{1,3,2,0:T(8,128)(2,1)S(1)} %bitcast.234, bf16[4,128,16,64]{1,3,2,0:T(8,128)(2,1)S(1)} %copy.58), kind=kOutput, calls=%fused_computation.12 | convolution fusion | flops 480763904 | bytes 34144256 | tf_op jit(solution)/shard_map/sqhe,skhe->shkq/dot_general | solution.py:182
  493.2 7.7 slice.255
  501.0 6.6 copy.81
  507.5 10.9 %multiply_convert_fusion.1 = bf16[4,16,448,128]{3,2,1,0:T(8,128)(2,1)S(1)} fusion(f32[4,16,448,128]{3,2,1,0:T(8,128)} %get-tuple-element.68, f32[4,16,448,128]{3,2,1,0:T(8,128)} %get-tuple-element.60, f32[4,16,128]{2,1,0:T(8,128)S(1)} %get-tuple-element.67, f32[4,16,128]{2,1,0:T(8,128)S(1)} %copy-done.31), kind=kLoop, calls=%fused_computation.11 | loop fusion | flops 14680064 | bytes 36765696 | tf_op jit(solution)/shard_map/convert_element_type | solution.py:186
  525.1 4.3 slice.254
  529.4 6.6 copy.80
  536.0 8.2 fusion.3
  544.2 5.0 fusion.400
  554.1 35.5 %all-gather.5 = bf16[1,4096]{1,0:T(2,128)(2,1)S(1)} all-gather(bf16[1,512]{1,0:T(2,128)(2,1)S(1)} %copy-done.40), channel_id=7, replica_groups=mesh['rows'=4,'wide'=8] {'wide'}, dimensions={1}, use_global_device_ids=true | all-gather | bytes 9216 | tf_op jit(solution)/shard_map/all_gather | solution.py:166
  589.7 4.8 fusion.238
  602.5 6.7 multiply_reduce_fusion.3
  611.2 37.1 %multiply_reduce_fusion.2 = (f32[512]{0:T(512)S(1)}, f32[512,1024]{1,0:T(8,128)}) fusion(f32[512,1024]{1,0:T(8,128)S(1)} %copy-done.14, f32[512]{0:T(512)S(1)} %copy-done.43, f32[1024]{0:T(1024)S(1)} %bitcast.263, bf16[1,4096,1024]{2,1,0:T(8,128)(2,1)} %all-gather.11.cloned.1.call-done, f32[512,4096]{1,0:T(8,128)} %fusion.36, f32[4096]{0:T(1024)S(1)} %bitcast.254, ...), kind=kOutput, calls=%fused_computation.254 | convolution fusion | flops 8747220992 | bytes 31483904 | tf_op jit(solution)/shard_map/dot_general | solution.py:50
  657.9 11.9 %fusion.66 = f32[4,16,64,448]{3,2,1,0:T(8,128)} fusion(bf16[4,128,16,64]{1,3,2,0:T(8,128)(2,1)S(1)} %copy.65, f32[4,16,448,128]{3,2,1,0:T(8,128)} %get-tuple-element.54, f32[4,16,128]{2,1,0:T(8,128)S(1)} %log_add_fusion), kind=kOutput, calls=%fused_computation.122 | convolution fusion | flops 477102080 | bytes 23101440 | tf_op jit(solution)/shard_map/shkq,sqhe->skhe/dot_general | solution.py:195
  669.7 10.2 %multiply_reduce_fusion = (f32[4,16,128]{2,1,0:T(8,128)S(1)}, f32[4,16,448,128]{3,2,1,0:T(8,128)}) fusion(f32[4,16,448,128]{3,2,1,0:T(8,128)} %get-tuple-element.54, f32[4,16,128]{2,1,0:T(8,128)S(1)} %log_add_fusion, bf16[4,448,16,64]{1,3,2,0:T(8,128)(2,1)S(1)} %bitcast.232, bf16[4,128,16,64]{1,3,2,0:T(8,128)(2,1)S(1)} %copy.65), kind=kOutput, calls=%fused_computation.9 | convolution fusion | flops 480763904 | bytes 34144256 | tf_op jit(solution)/shard_map/sqhe,skhe->shkq/dot_general | solution.py:182
  679.9 7.6 slice.261
  687.5 6.6 copy.83
  694.1 10.9 %multiply_convert_fusion = bf16[4,16,448,128]{3,2,1,0:T(8,128)(2,1)S(1)} fusion(f32[4,16,448,128]{3,2,1,0:T(8,128)} %get-tuple-element.74, f32[4,16,448,128]{3,2,1,0:T(8,128)} %get-tuple-element.54, f32[4,16,128]{2,1,0:T(8,128)S(1)} %get-tuple-element.73, f32[4,16,128]{2,1,0:T(8,128)S(1)} %log_add_fusion), kind=kLoop, calls=%fused_computation.8 | loop fusion | flops 14680064 | bytes 36765696 | tf_op jit(solution)/shard_map/convert_element_type | solution.py:186
  711.6 4.4 slice.260
  716.0 6.6 copy.82
  722.6 8.3 fusion.2
  730.8 4.9 fusion.399
  749.5 6.3 fusion.239
  759.2 123.3 %all-reduce.4.cloned.1.call-done = f32[2,2,64,1024]{2,3,1,0:T(8,128)} async-done(((f32[2,2,64,1024]{2,3,1,0:T(8,128)}), f32[2,2,64,1024]{2,3,1,0:T(8,128)}) %all-reduce.4.cloned.1.call-update) | async-done | bytes 1048592 | tf_op jit(solution)/shard_map/psum | solution.py:225
  889.7 7.5 add_add_fusion.8
  (322 shorter events, 156.1 us)
Async XLA Ops:
  7.2 171.1 %all-gather.11.cloned.1.call-start = ((), (), s32[]{:S(2)}) async-start(), calls=%async_computation.1 | async-start | bytes 9437184 | tf_op jit(solution)/shard_map/all_gather | solution.py:130
  10.4 192.2 %all-gather.13.cloned.1.call-start = ((), (), s32[]{:S(2)}) async-start(), calls=%async_computation.2 | async-start | bytes 9437184 | tf_op jit(solution)/shard_map/all_gather | solution.py:131
  13.5 370.5 %all-gather.15.cloned.1.call-start = ((), (), s32[]{:S(2)}) async-start(), calls=%async_computation.3 | async-start | bytes 9437184 | tf_op jit(solution)/shard_map/all_gather | solution.py:130
  14.2 380.1 %all-gather.17.cloned.1.call-start = ((), (), s32[]{:S(2)}) async-start(), calls=%async_computation.4 | async-start | bytes 9437184 | tf_op jit(solution)/shard_map/all_gather | solution.py:131
  14.9 83.2 %copy-start.62 = (f32[2,1024]{1,0:T(2,128)S(1)}, f32[2,1024]{1,0:T(2,128)}, u32[]{:S(2)}) copy-start(f32[2,1024]{1,0:T(2,128)} %param.25) | copy-start | bytes 24580
  23.2 102.7 %collective-permute-start.1 = (bf16[4,128,2048]{2,1,0:T(8,128)(2,1)S(1)}, bf16[4,128,2048]{2,1,0:T(8,128)(2,1)}, u32[]{:S(2)}, u32[]{:S(2)}) collective-permute-start(bf16[4,128,2048]{2,1,0:T(8,128)(2,1)S(1)} %slice.246), channel_id=1, source_target_pairs={{1,0},{2,1},{3,2},{4,3},{5,4},{6,5},{7,6},{9,8},{10,9},{11,10},{12... | collective-permute-start | bytes 6291464 | tf_op jit(solution)/shard_map/ppermute | solution.py:26
  24.4 101.4 %collective-permute-start = (bf16[4,128,2048]{2,1,0:T(8,128)(2,1)S(1)}, bf16[4,128,2048]{2,1,0:T(8,128)(2,1)}, u32[]{:S(2)}, u32[]{:S(2)}) collective-permute-start(bf16[4,128,2048]{2,1,0:T(8,128)(2,1)S(1)} %slice.246), channel_id=1, source_target_pairs={{0,1},{1,2},{2,3},{3,4},{4,5},{5,6},{6,7},{8,9},{9,10},{10,11},{11... | collective-permute-start | bytes 6291464 | tf_op jit(solution)/shard_map/ppermute | solution.py:23
  29.9 95.3 %copy-start.39 = (bf16[1,512]{1,0:T(2,128)(2,1)}, bf16[1,512]{1,0:T(2,128)(2,1)S(1)}, u32[]{:S(2)}) copy-start(bf16[1,512]{1,0:T(2,128)(2,1)S(1)} %get-tuple-element.52) | copy-start | bytes 3076
  29.9 68.9 %collective-permute-start.6 = (bf16[512]{0:T(512)(128)(2,1)S(1)}, bf16[512]{0:T(512)(128)(2,1)S(1)}, u32[]{:S(2)}, u32[]{:S(2)}) collective-permute-start(bf16[512]{0:T(512)(128)(2,1)S(1)} %get-tuple-element.9), channel_id=1, source_target_pairs={{1,0},{2,1},{3,2},{4,3},{5,4},{6,5},{7,6},{0,7},{9,8},{10,9},{11,1... | collective-permute-start | bytes 3080 | tf_op jit(solution)/shard_map/ppermute | solution.py:140
  33.9 4.8 collective-permute-start.2
  34.0 848.5 %all-reduce.4.cloned.1.call-start = ((), (), s32[]{:S(2)}) async-start(), calls=%async_computation | async-start | bytes 4194304 | tf_op jit(solution)/shard_map/psum | solution.py:225
  38.8 60.2 %collective-permute-start.3 = (bf16[512]{0:T(512)(128)(2,1)S(1)}, bf16[512]{0:T(512)(128)(2,1)S(1)}, u32[]{:S(2)}, u32[]{:S(2)}) collective-permute-start(bf16[512]{0:T(512)(128)(2,1)S(1)} %collective-permute-done.2), channel_id=1, source_target_pairs={{0,1},{1,2},{2,3},{3,4},{4,5},{5,6},{6,7},{7,0},{8,9},{9,10},{10,1... | collective-permute-start | bytes 3080 | tf_op jit(solution)/shard_map/ppermute | solution.py:138
  98.8 15.9 %collective-permute-start.7 = (bf16[512]{0:T(512)(128)(2,1)S(1)}, bf16[512]{0:T(512)(128)(2,1)S(1)}, u32[]{:S(2)}, u32[]{:S(2)}) collective-permute-start(bf16[512]{0:T(512)(128)(2,1)S(1)} %collective-permute-done.6), channel_id=1, source_target_pairs={{1,0},{2,1},{3,2},{4,3},{5,4},{6,5},{7,6},{0,7},{9,8},{10,9},{11,1... | collective-permute-start | bytes 3080 | tf_op jit(solution)/shard_map/ppermute | solution.py:140
  99.0 19.7 %collective-permute-start.4 = (bf16[512]{0:T(512)(128)(2,1)S(1)}, bf16[512]{0:T(512)(128)(2,1)S(1)}, u32[]{:S(2)}, u32[]{:S(2)}) collective-permute-start(bf16[512]{0:T(512)(128)(2,1)S(1)} %collective-permute-done.3), channel_id=1, source_target_pairs={{0,1},{1,2},{2,3},{3,4},{4,5},{5,6},{6,7},{7,0},{8,9},{9,10},{10,1... | collective-permute-start | bytes 3080 | tf_op jit(solution)/shard_map/ppermute | solution.py:138
  114.7 9.2 %collective-permute-start.8 = (bf16[512]{0:T(512)(128)(2,1)S(1)}, bf16[512]{0:T(512)(128)(2,1)}, u32[]{:S(2)}, u32[]{:S(2)}) collective-permute-start(bf16[512]{0:T(512)(128)(2,1)S(1)} %collective-permute-done.7), channel_id=1, source_target_pairs={{1,0},{2,1},{3,2},{4,3},{5,4},{6,5},{7,6},{0,7},{9,8},{10,9},{11,1... | collective-permute-start | bytes 3080 | tf_op jit(solution)/shard_map/ppermute | solution.py:140
  118.6 5.9 collective-permute-start.5
  177.0 25.6 %copy-start.13 = (f32[512,1024]{1,0:T(8,128)}, f32[512,1024]{1,0:T(8,128)S(1)}, u32[]{:S(2)}) copy-start(f32[512,1024]{1,0:T(8,128)S(1)} %get-tuple-element.56) | copy-start | bytes 6291460
  177.0 25.5 %copy-start.42 = (f32[512]{0:T(512)}, f32[512]{0:T(512)S(1)}, u32[]{:S(2)}) copy-start(f32[512]{0:T(512)S(1)} %broadcast_multiply_fusion.5) | copy-start | bytes 6148
  178.3 24.3 %copy-start.57 = (f32[512]{0:T(512)}, f32[512]{0:T(512)S(1)}, u32[]{:S(2)}) copy-start(f32[512]{0:T(512)S(1)} %fusion.265) | copy-start | bytes 6148
  202.6 27.8 %copy-start.56 = (f32[1,3072]{1,0:T(1,128)S(1)}, f32[1,3072]{1,0:T(1,128)}, u32[]{:S(2)}) copy-start(f32[1,3072]{1,0:T(1,128)} %get-tuple-element.35) | copy-start | bytes 36868
  202.6 27.8 %copy-start.70 = (f32[1,1,1024]{2,1,0:T(1,128)S(1)}, f32[1,1,1024]{2,1,0:T(1,128)}, u32[]{:S(2)}) copy-start(f32[1,1,1024]{2,1,0:T(1,128)} %get-tuple-element.38) | copy-start | bytes 12292
  202.6 27.8 %copy-start.74 = (f32[1,1,1024]{2,1,0:T(1,128)S(1)}, f32[1,1,1024]{2,1,0:T(1,128)}, u32[]{:S(2)}) copy-start(f32[1,1,1024]{2,1,0:T(1,128)} %get-tuple-element.42) | copy-start | bytes 12292
  229.1 151.6 %copy-start.44 = (f32[512]{0:T(512)}, f32[512]{0:T(512)S(1)}, u32[]{:S(2)}) copy-start(f32[512]{0:T(512)S(1)} %broadcast_multiply_fusion.4) | copy-start | bytes 6148
  229.5 151.2 %copy-start.59 = (f32[512]{0:T(512)}, f32[512]{0:T(512)S(1)}, u32[]{:S(2)}) copy-start(f32[512]{0:T(512)S(1)} %fusion.266) | copy-start | bytes 6148
  230.4 75.3 %copy-start.41 = (bf16[1,512]{1,0:T(2,128)(2,1)S(1)}, bf16[1,512]{1,0:T(2,128)(2,1)}, u32[]{:S(2)}) copy-start(bf16[1,512]{1,0:T(2,128)(2,1)} %get-tuple-element.51) | copy-start | bytes 3076
  238.9 87.2 %collective-permute-start.10 = (bf16[4,128,2048]{2,1,0:T(8,128)(2,1)S(1)}, bf16[4,128,2048]{2,1,0:T(8,128)(2,1)}, u32[]{:S(2)}, u32[]{:S(2)}) collective-permute-start(bf16[4,128,2048]{2,1,0:T(8,128)(2,1)S(1)} %slice.250), channel_id=1, source_target_pairs={{1,0},{2,1},{3,2},{4,3},{5,4},{6,5},{7,6},{9,8},{10,9},{11,10},{12... | collective-permute-start | bytes 6291464 | tf_op jit(solution)/shard_map/ppermute | solution.py:26
  240.2 86.0 %collective-permute-start.9 = (bf16[4,128,2048]{2,1,0:T(8,128)(2,1)S(1)}, bf16[4,128,2048]{2,1,0:T(8,128)(2,1)}, u32[]{:S(2)}, u32[]{:S(2)}) collective-permute-start(bf16[4,128,2048]{2,1,0:T(8,128)(2,1)S(1)} %slice.250), channel_id=1, source_target_pairs={{0,1},{1,2},{2,3},{3,4},{4,5},{5,6},{6,7},{8,9},{9,10},{10,11},{11... | collective-permute-start | bytes 6291464 | tf_op jit(solution)/shard_map/ppermute | solution.py:23
  244.6 4.8 collective-permute-start.11
  245.0 54.5 %collective-permute-start.15 = (bf16[512]{0:T(512)(128)(2,1)S(1)}, bf16[512]{0:T(512)(128)(2,1)S(1)}, u32[]{:S(2)}, u32[]{:S(2)}) collective-permute-start(bf16[512]{0:T(512)(128)(2,1)S(1)} %copy-done.76), channel_id=1, source_target_pairs={{1,0},{2,1},{3,2},{4,3},{5,4},{6,5},{7,6},{0,7},{9,8},{10,9},{11,1... | collective-permute-start | bytes 3080 | tf_op jit(solution)/shard_map/ppermute | solution.py:140
  249.4 50.9 %collective-permute-start.12 = (bf16[512]{0:T(512)(128)(2,1)S(1)}, bf16[512]{0:T(512)(128)(2,1)S(1)}, u32[]{:S(2)}, u32[]{:S(2)}) collective-permute-start(bf16[512]{0:T(512)(128)(2,1)S(1)} %collective-permute-done.11), channel_id=1, source_target_pairs={{0,1},{1,2},{2,3},{3,4},{4,5},{5,6},{6,7},{7,0},{8,9},{9,10},{10,1... | collective-permute-start | bytes 3080 | tf_op jit(solution)/shard_map/ppermute | solution.py:138
  299.5 3.3 collective-permute-start.16
  300.3 5.4 collective-permute-start.13
  302.7 18.7 %collective-permute-start.17 = (bf16[512]{0:T(512)(128)(2,1)S(1)}, bf16[512]{0:T(512)(128)(2,1)S(1)}, u32[]{:S(2)}, u32[]{:S(2)}) collective-permute-start(bf16[512]{0:T(512)(128)(2,1)S(1)} %collective-permute-done.16), channel_id=1, source_target_pairs={{1,0},{2,1},{3,2},{4,3},{5,4},{6,5},{7,6},{0,7},{9,8},{10,9},{11,1... | collective-permute-start | bytes 3080 | tf_op jit(solution)/shard_map/ppermute | solution.py:140
  305.7 15.8 %collective-permute-start.14 = (bf16[512]{0:T(512)(128)(2,1)S(1)}, bf16[512]{0:T(512)(128)(2,1)S(1)}, u32[]{:S(2)}, u32[]{:S(2)}) collective-permute-start(bf16[512]{0:T(512)(128)(2,1)S(1)} %collective-permute-done.13), channel_id=1, source_target_pairs={{0,1},{1,2},{2,3},{3,4},{4,5},{5,6},{6,7},{7,0},{8,9},{9,10},{10,1... | collective-permute-start | bytes 3080 | tf_op jit(solution)/shard_map/ppermute | solution.py:138
  326.1 25.4 %copy-start.7 = (bf16[4,128,1024]{1,2,0:T(8,128)(2,1)}, bf16[4,128,1024]{1,2,0:T(8,128)(2,1)S(1)}, u32[]{:S(2)}) copy-start(bf16[4,128,1024]{1,2,0:T(8,128)(2,1)S(1)} %copy.55) | copy-start | bytes 3145732
  394.3 26.6 %copy-start.18 = (bf16[4,128,1024]{2,1,0:T(8,128)(2,1)S(1)}, bf16[4,128,1024]{2,1,0:T(8,128)(2,1)}, u32[]{:S(2)}) copy-start(bf16[4,128,1024]{2,1,0:T(8,128)(2,1)} %param.27) | copy-start | bytes 3145732
  394.3 26.6 %copy-start.36 = (f32[1,1,1024]{2,1,0:T(1,128)S(1)}, f32[1,1,1024]{2,1,0:T(1,128)}, u32[]{:S(2)}) copy-start(f32[1,1,1024]{2,1,0:T(1,128)} %get-tuple-element.37) | copy-start | bytes 12292
  394.3 27.4 %copy-start.52 = (f32[1,1,1024]{2,1,0:T(1,128)S(1)}, f32[1,1,1024]{2,1,0:T(1,128)}, u32[]{:S(2)}) copy-start(f32[1,1,1024]{2,1,0:T(1,128)} %get-tuple-element.41) | copy-start | bytes 12292
  424.3 37.3 %copy-start.51 = (f32[512]{0:T(512)S(1)}, f32[512]{0:T(512)}, u32[]{:S(2)}) copy-start(f32[512]{0:T(512)} %copy-done.50) | copy-start | bytes 6148
  544.2 45.5 %copy-start.33 = (f32[4,16,128]{2,1,0:T(8,128)S(1)}, f32[4,16,128]{2,1,0:T(8,128)}, u32[]{:S(2)}) copy-start(f32[4,16,128]{2,1,0:T(8,128)} %copy-done.32) | copy-start | bytes 98308
  544.2 45.5 %copy-start.35 = (f32[4,16,128]{2,1,0:T(8,128)S(1)}, f32[4,16,128]{2,1,0:T(8,128)}, u32[]{:S(2)}) copy-start(f32[4,16,128]{2,1,0:T(8,128)} %copy-done.34) | copy-start | bytes 98308
  544.2 45.5 %copy-start.4 = (bf16[4,448,1024]{1,2,0:T(8,128)(2,1)S(1)}, bf16[4,448,1024]{1,2,0:T(8,128)(2,1)}, u32[]{:S(2)}) copy-start(bf16[4,448,1024]{1,2,0:T(8,128)(2,1)} %copy.54) | copy-start | bytes 11010052
  549.2 48.6 %collective-permute-start.18 = (bf16[4,128,2048]{2,1,0:T(8,128)(2,1)}, bf16[4,128,2048]{2,1,0:T(8,128)(2,1)}, u32[]{:S(2)}, u32[]{:S(2)}) collective-permute-start(bf16[4,128,2048]{2,1,0:T(8,128)(2,1)} %get-tuple-element.20), channel_id=1, source_target_pairs={{0,1},{1,2},{2,3},{3,4},{4,5},{5,6},{6,7},{8,9},{9,10},{10,11},{11... | collective-permute-start | bytes 6291464 | tf_op jit(solution)/shard_map/ppermute | solution.py:23
  552.8 45.0 %collective-permute-start.19 = (bf16[4,128,2048]{2,1,0:T(8,128)(2,1)}, bf16[4,128,2048]{2,1,0:T(8,128)(2,1)}, u32[]{:S(2)}, u32[]{:S(2)}) collective-permute-start(bf16[4,128,2048]{2,1,0:T(8,128)(2,1)} %get-tuple-element.21), channel_id=1, source_target_pairs={{1,0},{2,1},{3,2},{4,3},{5,4},{6,5},{7,6},{9,8},{10,9},{11,10},{12... | collective-permute-start | bytes 6291464 | tf_op jit(solution)/shard_map/ppermute | solution.py:26
  611.2 37.1 %copy-start.47 = (f32[512]{0:T(512)S(1)}, f32[512]{0:T(512)}, u32[]{:S(2)}) copy-start(f32[512]{0:T(512)} %copy-done.46) | copy-start | bytes 6148
  611.2 37.2 %copy-start.58 = (f32[512]{0:T(512)S(1)}, f32[512]{0:T(512)}, u32[]{:S(2)}) copy-start(f32[512]{0:T(512)} %copy-done.57) | copy-start | bytes 6148
  735.8 149.9 %collective-permute-start.20 = (bf16[4,128,2048]{2,1,0:T(8,128)(2,1)}, bf16[4,128,2048]{2,1,0:T(8,128)(2,1)}, u32[]{:S(2)}, u32[]{:S(2)}) collective-permute-start(bf16[4,128,2048]{2,1,0:T(8,128)(2,1)} %get-tuple-element.18), channel_id=1, source_target_pairs={{0,1},{1,2},{2,3},{3,4},{4,5},{5,6},{6,7},{8,9},{9,10},{10,11},{11... | collective-permute-start | bytes 6291464 | tf_op jit(solution)/shard_map/ppermute | solution.py:23
  739.4 146.2 %collective-permute-start.21 = (bf16[4,128,2048]{2,1,0:T(8,128)(2,1)}, bf16[4,128,2048]{2,1,0:T(8,128)(2,1)}, u32[]{:S(2)}, u32[]{:S(2)}) collective-permute-start(bf16[4,128,2048]{2,1,0:T(8,128)(2,1)} %get-tuple-element.19), channel_id=1, source_target_pairs={{1,0},{2,1},{3,2},{4,3},{5,4},{6,5},{7,6},{9,8},{10,9},{11,10},{12... | collective-permute-start | bytes 6291464 | tf_op jit(solution)/shard_map/ppermute | solution.py:26
  (60 other events, 507.7 us)
Sparse Core Ops, SparseCore 0:
  10.5 101.7 all-gather.10
  114.5 85.6 all-gather.12
  201.8 90.9 all-gather.14
  294.8 86.2 all-gather.16
  749.7 132.7 all-reduce.3
